TPU v7x, 32 devices: a whole 2x2x4 slice. The times are simulated.
32 devices in a mesh: dp: 4 (over x, core), expert: 8 (over z, y).
Axes of the slice: x: 2, y: 2, z: 4, core: 2. Of those that a mesh axis runs over, the one named last changes fastest.
Arguments:
- tokens: bfloat16 [256, 7168], P('dp', 'expert'), parts along dimension 0, may hold values from -6 to 6
- routes: int32 [256, 8], P('dp'), parts along dimension 0, may hold values from 0 to 15, all different within a row; in each aligned block of 64 rows (0 to 63, 64 to 127, ...) at most 40 rows name the same one
- gate_values: bfloat16 [256, 8], P('dp'), parts along dimension 0, may hold values from 0.049804688 to 1
- gate_weight: bfloat16 [7168, 16384], P(None, 'expert'), may hold values from -0.0625 to 0.0625
- up_weight: bfloat16 [7168, 16384], P(None, 'expert'), may hold values from -0.0625 to 0.0625
- down_weight: bfloat16 [16384, 7168], P(None, 'expert'), may hold values from -0.1875 to 0.1875
Outputs:
- layer_output: bfloat16 [256, 7168], P('dp', 'expert'), parts along dimension 0
There are 4 independent parts, one for each index of `dp`. A program takes and returns all parts, laid end to end along the dimension named above; an argument that names none is the same for every part. Nothing has to cross between parts.
Inputs may be any that keep to these rules, and one draw needn't show every extreme that they name: `routes`: each row names 8 different experts; no expert is named by more than 40 rows of a group, a bound that some block reaches.
All inputs are finite; a program needn't handle non-finite values.
Results may differ from a plain program's by a relative error of at most 0.0049.
Values may be sent and summed in bfloat16 or wider, within the bound.
A program may use at most 128 MiB of HBM per device.

v0:
```python
import jax
import jax.numpy as jnp
from jax import lax
from jax.sharding import PartitionSpec as P

HIDDEN_SIZE = 1024
EXPERTS = 16


def body(tokens, routes, gate_values, gate_weight, up_weight, down_weight):
    unit_count = gate_weight.shape[1]
    span_units = min(unit_count, HIDDEN_SIZE)
    local_count = unit_count // span_units
    token_count = tokens.shape[0]
    first_expert = lax.axis_index("expert") * unit_count // HIDDEN_SIZE
    matched = routes[:, :, None] == lax.broadcasted_iota(jnp.int32, (1, 1, EXPERTS), 2)
    combine_table = jnp.sum(
        jnp.where(matched, gate_values[:, :, None].astype(jnp.float32), 0.0), axis=1
    )
    selector = (
        lax.broadcasted_iota(jnp.int32, (EXPERTS, local_count), 0)
        == first_expert + lax.broadcasted_iota(jnp.int32, (EXPERTS, local_count), 1)
    ).astype(jnp.float32)
    local_gates = jnp.dot(
        combine_table, selector, precision=lax.Precision.HIGHEST, preferred_element_type=jnp.float32
    )
    all_rows = lax.all_gather(tokens, "expert", axis=1, tiled=True)
    gate_proj = jnp.dot(all_rows, gate_weight, preferred_element_type=jnp.float32)
    up_proj = jnp.dot(all_rows, up_weight, preferred_element_type=jnp.float32)
    product = (jax.nn.silu(gate_proj) * up_proj).reshape(token_count, local_count, span_units)
    product = product * local_gates[:, :, None]
    hidden = product.reshape(token_count, unit_count).astype(jnp.bfloat16)
    result = jnp.dot(
        lax.all_gather(hidden, "expert", axis=1, tiled=True),
        down_weight,
        preferred_element_type=jnp.float32,
    )
    return result.astype(jnp.bfloat16)


def solution(mesh):
    in_specs = (
        P("dp", "expert"),
        P("dp", None),
        P("dp", None),
        P(None, "expert"),
        P(None, "expert"),
        P(None, "expert"),
    )
    out_specs = P("dp", "expert")
    return jax.shard_map(body, mesh=mesh, in_specs=in_specs, out_specs=out_specs, check_vma=False)
```

profile of v0, /device:TPU:0, one launch (start us, length us, event | category | flops | bytes accessed | tf_op | source)
XLA Modules:
  0.0 140.3 jit_solution(4098790935787080068)
XLA Ops:
  6.5 0.0 all-gather.2.cloned.1.call-start
  6.5 0.7 convert_element_type.11
  7.2 0.7 select_reduce_fusion
  7.9 0.2 fusion.2
  8.2 0.2 mul.24
  8.4 0.2 copy.12
  8.5 34.4 %all_gather.6 = bf16[64,7168]{1,0:T(8,128)(2,1)S(1)} all-gather(bf16[64,896]{1,0:T(8,128)(2,1)} %param.6), channel_id=1, replica_groups=mesh['dp'=4,'expert'=8] {'expert'}, dimensions={1}, use_global_device_ids=true | all-gather | bytes 1032192 | tf_op jit(solution)/shard_map/all_gather | solution.py:27
  42.9 12.1 %fusion.4 = f32[64,2048]{1,0:T(8,128)S(1)} fusion(bf16[64,7168]{1,0:T(8,128)(2,1)S(1)} %all_gather.6, bf16[7168,2048]{1,0:T(8,128)(2,1)} %param.9), kind=kOutput, calls=%fused_computation.10 | convolution fusion | flops 1879048192 | bytes 30801920 | tf_op jit(solution)/shard_map/dot_general | solution.py:28
  55.0 12.9 %fusion.1 = bf16[64,2048]{1,0:T(8,128)(2,1)} fusion(f32[64,2048]{1,0:T(8,128)S(1)} %bitcast.9, bf16[64,7168]{1,0:T(8,128)(2,1)S(1)} %all_gather.6, bf16[7168,2048]{1,0:T(8,128)(2,1)} %param.10, f32[64,2048]{1,0:T(8,128)S(1)} %fusion.4), kind=kOutput, calls=%fused_computation.2 | convolution fusion | flops 1879965696 | bytes 31588352 | tf_op jit(solution)/shard_map/dot_general | solution.py:29
  67.9 0.0 all-gather.2.cloned.1.call-update
  67.9 50.2 %all-gather.2.cloned.1.call-done = bf16[64,16384]{1,0:T(8,128)(2,1)} async-done(((bf16[64,2048]{1,0:T(8,128)(2,1)}), bf16[64,16384]{1,0:T(8,128)(2,1)}) %all-gather.2.cloned.1.call-update) | async-done | bytes 2097168 | tf_op jit(solution)/shard_map/all_gather | solution.py:34
  118.2 15.3 %convolution_convert_fusion = bf16[64,896]{1,0:T(8,128)(2,1)} fusion(bf16[64,16384]{1,0:T(8,128)(2,1)} %all-gather.2.cloned.1.call-done, bf16[16384,896]{1,0:T(8,128)(2,1)} %param.11), kind=kOutput, calls=%fused_computation.3 | convolution fusion | flops 1879105536 | bytes 31571968 | tf_op jit(solution)/shard_map/dot_general | solution.py:33
  (1 shorter events, 0.0 us)
Async XLA Ops:
  6.5 111.6 %all-gather.2.cloned.1.call-start = ((), (), s32[]{:S(2)}) async-start(), calls=%async_computation | async-start | bytes 2359296 | tf_op jit(solution)/shard_map/all_gather | solution.py:34
Sparse Core Ops, SparseCore 0:
  68.1 50.0 all-gather.1
where the time goes:
time: 140 us
  waiting for transfers between devices  50.3 us (36%)
  matrix products  40.5 us (29%)
  blocking collectives  34.4 us (25%)
  between operations  13.4 us (10%)
    all_gather x1, waiting for transfers between devices, body(): lax.all_gather(hidden, 'expert', axis=1, tiled=True)  50.2 us
    all_gather x1, blocking collectives, body(): all_rows = lax.all_gather(tokens, 'expert', axis=1, tiled=True)  34.4 us
    dot_general x1, matrix products, body(): jnp.dot(lax.all_gather(hidden, 'expert', axis=1, tiled=True), down_weight...  15.3 us
    dot_general x1, matrix products, body(): up_proj = jnp.dot(all_rows, up_weight, preferred_element_type=jnp.float32)  12.9 us
    dot_general x1, matrix products, body(): jnp.dot(all_rows, gate_weight, preferred_element_type=jnp.float32)  12.1 us
  transfers between devices with their start and end apart: 1, of which 1 were waited for; matrix products, arithmetic and copies ran while one was open for 0% of the time, Pallas kernels for 0%

commit v1 on v0

--- a/solution.py
+++ b/solution.py
@@ -5,6 +5,13 @@
 
 HIDDEN_SIZE = 1024
 EXPERTS = 16
+
+
+def exchange_gather(block, mesh_axis, along):
+    size = lax.axis_size(mesh_axis)
+    tiles = jnp.stack([block for _ in range(size)])
+    tiles = lax.all_to_all(tiles, mesh_axis, split_axis=0, concat_axis=0)
+    return jnp.concatenate(tiles, axis=along)
 
 
 def body(tokens, routes, gate_values, gate_weight, up_weight, down_weight):
@@ -31,9 +38,7 @@
     product = product * local_gates[:, :, None]
     hidden = product.reshape(token_count, unit_count).astype(jnp.bfloat16)
     result = jnp.dot(
-        lax.all_gather(hidden, "expert", axis=1, tiled=True),
-        down_weight,
-        preferred_element_type=jnp.float32,
+        exchange_gather(hidden, "expert", 1), down_weight, preferred_element_type=jnp.float32
     )
     return result.astype(jnp.bfloat16)
 

time: 140 us -> 122 us (0.87)
  waiting for transfers between devices: 50.3 us -> 0 us
  blocking collectives: 34.4 us -> 82.3 us
  between operations: 13.4 us -> 0.05 us
  matrix products: 40.5 us -> 36.9 us
    all_gather x1 -> x0, waiting for transfers between devices: 50.2 us -> none  [body(): lax.all_gather(hidden, 'expert', axis=1, tiled=True)]
    all_to_all x0 -> x1, blocking collectives: none -> 47.9 us  [exchange_gather(): tiles = lax.all_to_all(tiles, mesh_axis, split_axis=0, concat_axis=0)]
    dot_general x1, matrix products: 15.3 us -> 12.4 us  [body(): jnp.dot(exchange_gather(hidden, 'expert', 1), down_weight, preferred_elem...]
  transfers between devices with their start and end apart: 1 -> 0, of which waited for: 1 -> 0; matrix products, arithmetic and copies ran while one was open for 0% -> 0% of each run, Pallas kernels for 0% -> 0%
where the time goes in v1:
time: 122 us; the launch traced here: 121 us
  blocking collectives  82.3 us (67%)
  matrix products  36.9 us (30%)
  other arithmetic  1.39 us (1%)
    all_to_all x1, blocking collectives, exchange_gather(): tiles = lax.all_to_all(tiles, mesh_axis, split_axis=0, concat_axis=0)  47.9 us
    all_gather x1, blocking collectives, body(): all_rows = lax.all_gather(tokens, 'expert', axis=1, tiled=True)  34.4 us
    dot_general x1, matrix products, body(): jnp.dot(exchange_gather(hidden, 'expert', 1), down_weight, preferred_elem...  12.4 us
    dot_general x1, matrix products, body(): up_proj = jnp.dot(all_rows, up_weight, preferred_element_type=jnp.float32)  12.2 us
    dot_general x1, matrix products, body(): jnp.dot(all_rows, gate_weight, preferred_element_type=jnp.float32)  12.1 us

profile of v1, /device:TPU:0, one launch (start us, length us, event | category | flops | bytes accessed | tf_op | source)
XLA Modules:
  0.0 121.4 jit_solution(4496944814511926825)
XLA Ops:
  0.0 0.7 convert_element_type.11
  0.7 0.7 select_reduce_fusion
  1.4 0.2 fusion.2
  1.6 0.2 mul.24
  1.8 0.2 copy.21
  2.0 34.4 %all_gather.3 = bf16[64,7168]{1,0:T(8,128)(2,1)S(1)} all-gather(bf16[64,896]{1,0:T(8,128)(2,1)} %param.6), channel_id=1, replica_groups=mesh['dp'=4,'expert'=8] {'expert'}, dimensions={1}, use_global_device_ids=true | all-gather | bytes 1032192 | tf_op jit(solution)/shard_map/all_gather | solution.py:34
  36.4 12.1 %fusion.4 = f32[64,2048]{1,0:T(8,128)S(1)} fusion(bf16[64,7168]{1,0:T(8,128)(2,1)S(1)} %all_gather.3, bf16[7168,2048]{1,0:T(8,128)(2,1)} %param.9), kind=kOutput, calls=%fused_computation.10 | convolution fusion | flops 1879048192 | bytes 30801920 | tf_op jit(solution)/shard_map/dot_general | solution.py:35
  48.4 12.2 %fusion.1 = bf16[64,2048]{1,0:T(8,128)(2,1)S(1)} fusion(f32[64,2048]{1,0:T(8,128)S(1)} %bitcast.14, bf16[64,7168]{1,0:T(8,128)(2,1)S(1)} %all_gather.3, bf16[7168,2048]{1,0:T(8,128)(2,1)} %param.10, f32[64,2048]{1,0:T(8,128)S(1)} %fusion.4), kind=kOutput, calls=%fused_computation.2 | convolution fusion | flops 1879965696 | bytes 31588352 | tf_op jit(solution)/shard_map/dot_general | solution.py:36
  60.7 0.2 stack.2
  60.9 47.9 %all_to_all.5 = bf16[8,64,2048]{2,1,0:T(8,128)(2,1)S(1)} all-to-all(bf16[8,64,2048]{2,1,0:T(8,128)(2,1)S(1)} %stack.2), channel_id=1, replica_groups=mesh['dp'=4,'expert'=8] {'expert'}, dimensions={0} | all-to-all | bytes 4194304 | tf_op jit(solution)/shard_map/all_to_all | solution.py:13
  108.8 0.1 copy.20
  108.9 12.4 %convolution_convert_fusion = bf16[64,896]{1,0:T(8,128)(2,1)} fusion(bf16[64,16384]{1,0:T(8,128)(2,1)S(1)} %bitcast.12, bf16[16384,896]{1,0:T(8,128)(2,1)} %param.11), kind=kOutput, calls=%fused_computation.3 | convolution fusion | flops 1879105536 | bytes 31571968 | tf_op jit(solution)/shard_map/dot_general | solution.py:40
  (1 shorter events, 0.0 us)
